TPU v7x, 16 devices: a whole 2x2x2 slice. The times are simulated.
16 devices in a mesh: dp: 2 (over z), cp: 8 (over y, x, core).
Axes of the slice: x: 2, y: 2, z: 2, core: 2. Of those that a mesh axis runs over, the one named last changes fastest.
Arguments:
- x: bfloat16 [4096, 5376], P(('dp', 'cp')), parts along dimension 0
- wq: bfloat16 [6, 5376, 32, 128], replicated
- wk: bfloat16 [6, 5376, 16, 128], replicated
- wv: bfloat16 [6, 5376, 16, 128], replicated
- wo: bfloat16 [6, 32, 128, 5376], replicated
Outputs:
- output: bfloat16 [4096, 5376], P(('dp', 'cp')), parts along dimension 0
There are 2 independent parts. A program takes and returns all parts, laid end to end along the dimension named above; an argument that names none is the same for every part.
All inputs are finite; a program needn't handle non-finite values.
Results may differ from a plain program's by a relative error of at most 0.0118365.
Values are sent between devices in bfloat16 or wider.
A program may use at most 3 GiB of HBM per device.

v0:
```python
import jax
import jax.numpy as jnp
from jax import lax
from jax.sharding import PartitionSpec as P

WINDOW = 1024
NEG = -1e30


def rms_norm(x):
    xf = x.astype(jnp.float32)
    return (xf * lax.rsqrt(jnp.mean(xf * xf, axis=-1, keepdims=True) + 1e-6)).astype(jnp.bfloat16)


def earlier_keys(a, n, t, window):
    reach = -(-window // t)
    hops = min(reach, n - 1)
    pieces = []
    for j in range(hops, 0, -1):
        src = a
        if j == reach:
            src = a[t - (window - (reach - 1) * t):]
        pieces.append(lax.ppermute(src, 'cp', [(s, s + j) for s in range(n - j)]))
    pieces.append(a)
    have = sum(piece.shape[0] for piece in pieces)
    out = jnp.concatenate(pieces, axis=0)
    if have < window + t:
        out = jnp.pad(out, ((window + t - have, 0), (0, 0), (0, 0)))
    return out


def local_attention(q, k, v, first, window):
    t, kvh, grp, hd = q.shape
    qb = min(t, 256)
    nb = t // qb
    span = window + qb
    scale = hd ** -0.5
    qr = q.reshape(nb, qb, kvh, grp, hd)

    def block(args):
        b, qblk = args
        ks = lax.dynamic_slice_in_dim(k, b * qb, span, axis=0)
        vs = lax.dynamic_slice_in_dim(v, b * qb, span, axis=0)
        qpos = first + b * qb + jnp.arange(qb)
        kpos = first - window + b * qb + jnp.arange(span)
        s = jnp.einsum('qhgd,khd->qhgk', qblk, ks, preferred_element_type=jnp.float32) * scale
        mask = (kpos[None, :] >= 0) & (kpos[None, :] <= qpos[:, None]) & (kpos[None, :] > qpos[:, None] - window)
        mask = mask[:, None, None, :]
        s = jnp.where(mask, s, NEG)
        mx = s.max(axis=-1, keepdims=True)
        pr = jnp.where(mask, jnp.exp(s - mx), 0.0)
        o = jnp.einsum('qhgk,khd->qhgd', pr.astype(vs.dtype), vs, preferred_element_type=jnp.float32)
        return o / pr.sum(axis=-1)[..., None]

    o = lax.map(block, (jnp.arange(nb), qr))
    return o.reshape(t, kvh * grp * hd).astype(jnp.bfloat16)


def block_update(carry, q, first, k, v, kfirst):
    nb, qb, kvh, grp, hd = q.shape
    scale = hd ** -0.5
    kpos = kfirst + jnp.arange(k.shape[0])

    def block(args):
        b, qblk, mb, lb, ab = args
        qpos = first + b * qb + jnp.arange(qb)
        s = jnp.einsum('qhgd,khd->qhgk', qblk, k, preferred_element_type=jnp.float32) * scale
        mask = (kpos[None, :] <= qpos[:, None])[:, None, None, :]
        s = jnp.where(mask, s, NEG)
        mn = jnp.maximum(mb, s.max(axis=-1))
        pr = jnp.where(mask, jnp.exp(s - mn[..., None]), 0.0)
        alpha = jnp.exp(mb - mn)
        ln = alpha * lb + pr.sum(axis=-1)
        an = alpha[..., None] * ab + jnp.einsum('qhgk,khd->qhgd', pr.astype(v.dtype), v, preferred_element_type=jnp.float32)
        return mn, ln, an

    m, l, acc = carry
    return lax.map(block, (jnp.arange(nb), q, m, l, acc))


def global_attention(q, k, v, r, n, first):
    t, kvh, grp, hd = q.shape
    qb = min(t, 256)
    nb = t // qb
    qr = q.reshape(nb, qb, kvh, grp, hd)
    carry = (jnp.full((nb, qb, kvh, grp), NEG, jnp.float32), jnp.zeros((nb, qb, kvh, grp), jnp.float32), jnp.zeros((nb, qb, kvh, grp, hd), jnp.float32))

    def use(c, kb, vb, kfirst):
        return block_update(c, qr, first, kb, vb, kfirst)

    def skip(c, kb, vb, kfirst):
        return c

    perm = [(s, (s + 1) % n) for s in range(n)]
    kb, vb = k, v
    for j in range(n):
        src = (r - j) % n
        carry = lax.cond(j <= r, use, skip, carry, kb, vb, src * t)
        if j < n - 1:
            kb = lax.ppermute(kb, 'cp', perm)
            vb = lax.ppermute(vb, 'cp', perm)
    m, l, acc = carry
    o = acc / l[..., None]
    return o.reshape(t, kvh * grp * hd).astype(jnp.bfloat16)


def solution(mesh):
    n = mesh.shape['cp']

    def body(x, wq, wk, wv, wo):
        t, dm = x.shape
        nl, _, heads, hd = wq.shape
        kvh = wk.shape[2]
        grp = heads // kvh
        r = lax.axis_index('cp')
        first = r * t
        for layer in range(nl):
            h = rms_norm(x)
            q = jnp.dot(h, wq[layer].reshape(dm, heads * hd), preferred_element_type=jnp.float32).astype(jnp.bfloat16).reshape(t, kvh, grp, hd)
            k = jnp.dot(h, wk[layer].reshape(dm, kvh * hd), preferred_element_type=jnp.float32).astype(jnp.bfloat16).reshape(t, kvh, hd)
            v = jnp.dot(h, wv[layer].reshape(dm, kvh * hd), preferred_element_type=jnp.float32).astype(jnp.bfloat16).reshape(t, kvh, hd)
            if layer < nl - 1:
                kw = earlier_keys(k, n, t, WINDOW)
                vw = earlier_keys(v, n, t, WINDOW)
                o = local_attention(q, kw, vw, first, WINDOW)
            else:
                o = global_attention(q, k, v, r, n, first)
            y = jnp.dot(o, wo[layer].reshape(heads * hd, dm), preferred_element_type=jnp.float32)
            x = (x.astype(jnp.float32) + y).astype(jnp.bfloat16)
        return x

    spec_x = P(('dp', 'cp'), None)
    return jax.shard_map(body, mesh=mesh, in_specs=(spec_x, P(), P(), P(), P()), out_specs=spec_x, check_vma=False)
```

profile of v0, /device:TPU:7, one launch (start us, length us, event | category | flops | bytes accessed | tf_op | source)
XLA Modules:
  0.0 1948.8 jit_solution(17306611353523544991)
XLA Ops:
  0.0 86.1 %fusion.462 = (bf16[1,5376,16,128]{3,2,1,0:T(8,128)(2,1)}, bf16[1,5376,16,128]{3,2,1,0:T(8,128)(2,1)}, bf16[1,5376,16,128]{3,2,1,0:T(8,128)(2,1)}, bf16[1,5376,1...) fusion(bf16[6,5376,16,128]{3,2,1,0:T(8,128)(2,1)} %param.23), kind=kLoop, calls=%fused_computation.515 | loop fusion | bytes 264241152 | tf_op jit(solution)/shard_map/slice | solution.py:120
  104.8 86.3 %fusion.461 = (bf16[1,5376,16,128]{3,2,1,0:T(8,128)(2,1)}, bf16[1,5376,16,128]{3,2,1,0:T(8,128)(2,1)}, bf16[1,5376,16,128]{3,2,1,0:T(8,128)(2,1)}, bf16[1,5376,1...) fusion(bf16[6,5376,16,128]{3,2,1,0:T(8,128)(2,1)} %param.24), kind=kLoop, calls=%fused_computation.514 | loop fusion | bytes 264241152 | tf_op jit(solution)/shard_map/slice | solution.py:121
  204.3 170.6 %fusion.460 = (bf16[1,5376,32,128]{3,2,1,0:T(8,128)(2,1)}, bf16[1,5376,32,128]{3,2,1,0:T(8,128)(2,1)}, bf16[1,5376,32,128]{3,2,1,0:T(8,128)(2,1)}, bf16[1,5376,3...) fusion(bf16[6,5376,32,128]{3,2,1,0:T(8,128)(2,1)} %param.22), kind=kLoop, calls=%fused_computation.513 | loop fusion | bytes 528482304 | tf_op jit(solution)/shard_map/slice | solution.py:119
  374.9 169.6 %fusion.459 = (bf16[1,32,128,5376]{3,2,1,0:T(8,128)(2,1)}, bf16[1,32,128,5376]{3,2,1,0:T(8,128)(2,1)}, bf16[1,32,128,5376]{3,2,1,0:T(8,128)(2,1)}, bf16[1,32,128...) fusion(bf16[6,32,128,5376]{3,2,1,0:T(8,128)(2,1)} %param.25), kind=kLoop, calls=%fused_computation.512 | loop fusion | bytes 528482304 | tf_op jit(solution)/shard_map/slice | solution.py:128
  602.9 23.1 %fusion.463 = (f32[256,16,2]{0,2,1:T(2,128)S(1)}, bf16[256,16,2,1280]{0,3,2,1:T(8,128)(2,1)}) fusion(pred[256,1280]{0,1:T(8,128)(4,1)S(1)} %compare_and_fusion, bf16[1280,16,128]{2,0,1:T(8,128)(2,1)} %copy-done.37, bf16[256,16,2,128]{3,2,1,0:T(2,128)(2,1)} %squeeze.174), kind=kOutput, calls=%fused_computation.516 | convolution fusion | flops 2747270400 | bytes 28672000 | tf_op jit(solution)/shard_map/while/body/eval_jaxpr/sub | solution.py:51
  638.8 22.6 %fusion.276 = (f32[256]{0:T(256)S(1)}, bf16[256,5376]{1,0:T(8,128)(2,1)}) fusion(bf16[256,4096]{0,1:T(8,128)(2,1)} %bitcast.821, bf16[4096,5376]{1,0:T(8,128)(2,1)} %bitcast.774, bf16[256,5376]{1,0:T(8,128)(2,1)S(1)} %copy-done.2), kind=kOutput, calls=%fused_computation.365 | convolution fusion | flops 11282546688 | bytes 51643392 | tf_op jit(solution)/shard_map/dot_general | solution.py:128
  764.3 33.6 %collective-permute-done.13 = bf16[256,16,128]{2,0,1:T(8,128)(2,1)} collective-permute-done((bf16[256,16,128]{2,0,1:T(8,128)(2,1)}, bf16[256,16,128]{2,0,1:T(8,128)(2,1)}, u32[]{:S(2)}, u32[]{:S(2)}) %collective-permute-start.13) | collective-permute-done | bytes 1048608 | tf_op jit(solution)/shard_map/ppermute | solution.py:23
  805.3 23.9 %fusion.468 = (f32[256,16,2]{0,2,1:T(2,128)S(1)}, bf16[256,16,2,1280]{0,3,2,1:T(8,128)(2,1)}) fusion(pred[256,1280]{0,1:T(8,128)(4,1)S(1)} %compare_and_fusion, bf16[1280,16,128]{2,0,1:T(8,128)(2,1)} %constant_dynamic-update-slice_fusion.15, bf16[256,16,2,128]{3,2,1,0:T(2,128)(2,1)S(1)} %squeeze.175), kind=kOutput, calls=%fused_computation.517 | convolution fusion | flops 2747270400 | bytes 28672000 | tf_op jit(solution)/shard_map/while/body/eval_jaxpr/sub | solution.py:51
  842.0 21.6 %fusion.278 = (f32[256]{0:T(256)S(1)}, bf16[256,5376]{1,0:T(8,128)(2,1)S(1)}) fusion(bf16[256,4096]{0,1:T(8,128)(2,1)} %bitcast.817, bf16[4096,5376]{1,0:T(8,128)(2,1)} %bitcast.773, bf16[256,5376]{1,0:T(8,128)(2,1)} %get-tuple-element.1050), kind=kOutput, calls=%fused_computation.367 | convolution fusion | flops 11282546688 | bytes 51643392 | tf_op jit(solution)/shard_map/dot_general | solution.py:128
  896.5 60.6 %collective-permute-done.16 = bf16[256,16,128]{0,2,1:T(8,128)(2,1)} collective-permute-done((bf16[256,16,128]{0,2,1:T(8,128)(2,1)}, bf16[256,16,128]{0,2,1:T(8,128)(2,1)}, u32[]{:S(2)}, u32[]{:S(2)}) %collective-permute-start.16) | collective-permute-done | bytes 1048608 | tf_op jit(solution)/shard_map/ppermute | solution.py:23
  995.8 36.7 %collective-permute-done.21 = bf16[256,16,128]{2,0,1:T(8,128)(2,1)} collective-permute-done((bf16[256,16,128]{2,0,1:T(8,128)(2,1)}, bf16[256,16,128]{2,0,1:T(8,128)(2,1)}, u32[]{:S(2)}, u32[]{:S(2)}) %collective-permute-start.21) | collective-permute-done | bytes 1048608 | tf_op jit(solution)/shard_map/ppermute | solution.py:23
  1039.8 23.3 %fusion.473 = (f32[256,16,2]{0,2,1:T(2,128)S(1)}, bf16[256,16,2,1280]{0,3,2,1:T(8,128)(2,1)}) fusion(pred[256,1280]{0,1:T(8,128)(4,1)S(1)} %compare_and_fusion, bf16[1280,16,128]{2,0,1:T(8,128)(2,1)} %constant_dynamic-update-slice_fusion.25, bf16[256,16,2,128]{3,2,1,0:T(2,128)(2,1)} %squeeze.176), kind=kOutput, calls=%fused_computation.518 | convolution fusion | flops 2747270400 | bytes 28672000 | tf_op jit(solution)/shard_map/while/body/eval_jaxpr/sub | solution.py:51
  1075.9 22.2 %fusion.280 = (f32[256]{0:T(256)S(1)}, bf16[256,5376]{1,0:T(8,128)(2,1)}) fusion(bf16[256,4096]{0,1:T(8,128)(2,1)} %bitcast.818, bf16[4096,5376]{1,0:T(8,128)(2,1)} %bitcast.772, bf16[256,5376]{1,0:T(8,128)(2,1)S(1)} %get-tuple-element.1054), kind=kOutput, calls=%fused_computation.369 | convolution fusion | flops 11282546688 | bytes 51643392 | tf_op jit(solution)/shard_map/dot_general | solution.py:128
  1131.8 62.2 %collective-permute-done.24 = bf16[256,16,128]{0,2,1:T(8,128)(2,1)S(1)} collective-permute-done((bf16[256,16,128]{0,2,1:T(8,128)(2,1)}, bf16[256,16,128]{0,2,1:T(8,128)(2,1)S(1)}, u32[]{:S(2)}, u32[]{:S(2)}) %collective-permute-start.24) | collective-permute-done | bytes 1048608 | tf_op jit(solution)/shard_map/ppermute | solution.py:23
  1231.5 37.2 %collective-permute-done.29 = bf16[256,16,128]{2,0,1:T(8,128)(2,1)} collective-permute-done((bf16[256,16,128]{2,0,1:T(8,128)(2,1)}, bf16[256,16,128]{2,0,1:T(8,128)(2,1)}, u32[]{:S(2)}, u32[]{:S(2)}) %collective-permute-start.29) | collective-permute-done | bytes 1048608 | tf_op jit(solution)/shard_map/ppermute | solution.py:23
  1276.0 24.1 %fusion.478 = (f32[256,16,2]{0,2,1:T(2,128)S(1)}, bf16[256,16,2,1280]{0,3,2,1:T(8,128)(2,1)}) fusion(pred[256,1280]{0,1:T(8,128)(4,1)S(1)} %compare_and_fusion, bf16[1280,16,128]{2,0,1:T(8,128)(2,1)} %constant_dynamic-update-slice_fusion.35, bf16[256,16,2,128]{3,2,1,0:T(2,128)(2,1)S(1)} %squeeze.177), kind=kOutput, calls=%fused_computation.519 | convolution fusion | flops 2747270400 | bytes 28672000 | tf_op jit(solution)/shard_map/while/body/eval_jaxpr/sub | solution.py:51
  1312.9 21.6 %fusion.282 = (f32[256]{0:T(256)S(1)}, bf16[256,5376]{1,0:T(8,128)(2,1)S(1)}) fusion(bf16[256,4096]{0,1:T(8,128)(2,1)} %bitcast.819, bf16[4096,5376]{1,0:T(8,128)(2,1)} %bitcast.771, bf16[256,5376]{1,0:T(8,128)(2,1)} %get-tuple-element.1058), kind=kOutput, calls=%fused_computation.371 | convolution fusion | flops 11282546688 | bytes 51643392 | tf_op jit(solution)/shard_map/dot_general | solution.py:128
  1368.2 60.7 %collective-permute-done.32 = bf16[256,16,128]{0,2,1:T(8,128)(2,1)S(1)} collective-permute-done((bf16[256,16,128]{0,2,1:T(8,128)(2,1)}, bf16[256,16,128]{0,2,1:T(8,128)(2,1)S(1)}, u32[]{:S(2)}, u32[]{:S(2)}) %collective-permute-start.32) | collective-permute-done | bytes 1048608 | tf_op jit(solution)/shard_map/ppermute | solution.py:23
  1466.7 36.9 %collective-permute-done.37 = bf16[256,16,128]{2,0,1:T(8,128)(2,1)} collective-permute-done((bf16[256,16,128]{2,0,1:T(8,128)(2,1)}, bf16[256,16,128]{2,0,1:T(8,128)(2,1)}, u32[]{:S(2)}, u32[]{:S(2)}) %collective-permute-start.37) | collective-permute-done | bytes 1048608 | tf_op jit(solution)/shard_map/ppermute | solution.py:23
  1511.0 24.0 %fusion.483 = (f32[256,16,2]{0,2,1:T(2,128)S(1)}, bf16[256,16,2,1280]{0,3,2,1:T(8,128)(2,1)}) fusion(pred[256,1280]{0,1:T(8,128)(4,1)S(1)} %compare_and_fusion, bf16[1280,16,128]{2,0,1:T(8,128)(2,1)} %constant_dynamic-update-slice_fusion.45, bf16[256,16,2,128]{3,2,1,0:T(2,128)(2,1)S(1)} %squeeze.178), kind=kOutput, calls=%fused_computation.520 | convolution fusion | flops 2747270400 | bytes 28672000 | tf_op jit(solution)/shard_map/while/body/eval_jaxpr/sub | solution.py:51
  1547.8 21.5 %fusion.284 = (f32[256]{0:T(256)S(1)}, bf16[256,5376]{1,0:T(8,128)(2,1)S(1)}) fusion(bf16[256,4096]{0,1:T(8,128)(2,1)} %bitcast.820, bf16[4096,5376]{1,0:T(8,128)(2,1)} %bitcast.770, bf16[256,5376]{1,0:T(8,128)(2,1)} %copy-done.5), kind=kOutput, calls=%fused_computation.373 | convolution fusion | flops 11282546688 | bytes 51643392 | tf_op jit(solution)/shard_map/dot_general | solution.py:128
  1591.9 54.4 %collective-permute-start.41 = (bf16[256,16,128]{2,0,1:T(8,128)(2,1)S(1)}, bf16[256,16,128]{2,0,1:T(8,128)(2,1)S(1)}, u32[]{:S(2)}, u32[]{:S(2)}) collective-permute-start(bf16[256,16,128]{2,0,1:T(8,128)(2,1)S(1)} %copy_bitcast_fusion), channel_id=1, source_target_pairs={{0,1},{1,2},{2,3},{3,4},{4,5},{5,6},{6,7},{7,0},{8,9},{9,10},{10,1... | collective-permute-start | bytes 3145736 | tf_op jit(solution)/shard_map/ppermute | solution.py:101
  1898.5 24.0 %conditional.15 = (f32[1,256,16,2]{1,3,2,0:T(2,128)S(1)}, f32[1,256,16,2,128]{1,4,3,2,0:T(8,128)}) conditional(s32[]{:T(128)} %convert_element_type.276, (f32[1,256,16,2]{1,3,2,0:T(2,128)S(1)}, f32[1,256,16,2,128]{4,1,3,2,0:T(8,128)}) %tuple.100, (s32[]{:T(128)}, s32[]{:T(128)}, bf16[1,256,16,2,128]{4,3,2,1,0:T(2,128)(2,1)S(1)}, ...), branch_computations={%region_44.45_spmd, %region_45.48_spmd.clone} | conditional | flops 1103200768 | bytes 80416952 | solution.py:98
  1926.7 21.8 %fusion.273 = bf16[256,5376]{1,0:T(8,128)(2,1)} fusion(bf16[256,4096]{0,1:T(8,128)(2,1)} %bitcast.793, bf16[4096,5376]{1,0:T(8,128)(2,1)} %bitcast.769, bf16[256,5376]{1,0:T(8,128)(2,1)S(1)} %copy-done.4), kind=kOutput, calls=%fused_computation.362 | convolution fusion | flops 11278417920 | bytes 51642368 | tf_op jit(solution)/shard_map/dot_general | solution.py:128
  (373 shorter events, 889.6 us)
Async XLA Ops:
  99.4 464.1 %collective-permute-start.4 = (bf16[256,16,128]{2,0,1:T(8,128)(2,1)}, bf16[256,16,128]{2,0,1:T(8,128)(2,1)}, u32[]{:S(2)}, u32[]{:S(2)}) collective-permute-start(bf16[256,16,128]{2,0,1:T(8,128)(2,1)} %bitcast.768), channel_id=1, source_target_pairs={{0,4},{1,5},{2,6},{3,7},{8,12},{9,13},{10,14},{11,15}} | collective-permute-start | bytes 3145736 | tf_op jit(solution)/shard_map/ppermute | solution.py:23
  100.7 464.1 %collective-permute-start.5 = (bf16[256,16,128]{2,0,1:T(8,128)(2,1)}, bf16[256,16,128]{2,0,1:T(8,128)(2,1)}, u32[]{:S(2)}, u32[]{:S(2)}) collective-permute-start(bf16[256,16,128]{2,0,1:T(8,128)(2,1)} %bitcast.768), channel_id=1, source_target_pairs={{0,3},{1,4},{2,5},{3,6},{4,7},{8,11},{9,12},{10,13},{11,14},{12,15}} | collective-permute-start | bytes 3145736 | tf_op jit(solution)/shard_map/ppermute | solution.py:23
  102.0 476.3 %collective-permute-start.6 = (bf16[256,16,128]{2,0,1:T(8,128)(2,1)}, bf16[256,16,128]{2,0,1:T(8,128)(2,1)}, u32[]{:S(2)}, u32[]{:S(2)}) collective-permute-start(bf16[256,16,128]{2,0,1:T(8,128)(2,1)} %bitcast.768), channel_id=1, source_target_pairs={{0,2},{1,3},{2,4},{3,5},{4,6},{5,7},{8,10},{9,11},{10,12},{11,13},... | collective-permute-start | bytes 3145736 | tf_op jit(solution)/shard_map/ppermute | solution.py:23
  103.3 476.4 %collective-permute-start.7 = (bf16[256,16,128]{2,0,1:T(8,128)(2,1)}, bf16[256,16,128]{2,0,1:T(8,128)(2,1)}, u32[]{:S(2)}, u32[]{:S(2)}) collective-permute-start(bf16[256,16,128]{2,0,1:T(8,128)(2,1)} %bitcast.768), channel_id=1, source_target_pairs={{0,1},{1,2},{2,3},{3,4},{4,5},{5,6},{6,7},{8,9},{9,10},{10,11},{11... | collective-permute-start | bytes 3145736 | tf_op jit(solution)/shard_map/ppermute | solution.py:23
  202.8 370.1 %collective-permute-start = (bf16[256,16,128]{0,2,1:T(8,128)(2,1)}, bf16[256,16,128]{0,2,1:T(8,128)(2,1)}, u32[]{:S(2)}, u32[]{:S(2)}) collective-permute-start(bf16[256,16,128]{0,2,1:T(8,128)(2,1)} %bitcast.145), channel_id=1, source_target_pairs={{0,4},{1,5},{2,6},{3,7},{8,12},{9,13},{10,14},{11,15}} | collective-permute-start | bytes 3145736 | tf_op jit(solution)/shard_map/ppermute | solution.py:23
  679.6 79.8 %collective-permute-start.11 = (bf16[256,16,128]{0,2,1:T(8,128)(2,1)}, bf16[256,16,128]{0,2,1:T(8,128)(2,1)}, u32[]{:S(2)}, u32[]{:S(2)}) collective-permute-start(bf16[256,16,128]{0,2,1:T(8,128)(2,1)} %bitcast.799), channel_id=1, source_target_pairs={{0,1},{1,2},{2,3},{3,4},{4,5},{5,6},{6,7},{8,9},{9,10},{10,11},{11... | collective-permute-start | bytes 3145736 | tf_op jit(solution)/shard_map/ppermute | solution.py:23
  711.6 86.4 %collective-permute-start.13 = (bf16[256,16,128]{2,0,1:T(8,128)(2,1)}, bf16[256,16,128]{2,0,1:T(8,128)(2,1)}, u32[]{:S(2)}, u32[]{:S(2)}) collective-permute-start(bf16[256,16,128]{2,0,1:T(8,128)(2,1)} %bitcast.767), channel_id=1, source_target_pairs={{0,3},{1,4},{2,5},{3,6},{4,7},{8,11},{9,12},{10,13},{11,14},{12,15}} | collective-permute-start | bytes 3145736 | tf_op jit(solution)/shard_map/ppermute | solution.py:23
  877.0 80.2 %collective-permute-start.16 = (bf16[256,16,128]{0,2,1:T(8,128)(2,1)}, bf16[256,16,128]{0,2,1:T(8,128)(2,1)}, u32[]{:S(2)}, u32[]{:S(2)}) collective-permute-start(bf16[256,16,128]{0,2,1:T(8,128)(2,1)} %bitcast.801), channel_id=1, source_target_pairs={{0,4},{1,5},{2,6},{3,7},{8,12},{9,13},{10,14},{11,15}} | collective-permute-start | bytes 3145736 | tf_op jit(solution)/shard_map/ppermute | solution.py:23
  878.2 82.4 %collective-permute-start.17 = (bf16[256,16,128]{0,2,1:T(8,128)(2,1)}, bf16[256,16,128]{0,2,1:T(8,128)(2,1)}, u32[]{:S(2)}, u32[]{:S(2)}) collective-permute-start(bf16[256,16,128]{0,2,1:T(8,128)(2,1)} %bitcast.802), channel_id=1, source_target_pairs={{0,3},{1,4},{2,5},{3,6},{4,7},{8,11},{9,12},{10,13},{11,14},{12,15}} | collective-permute-start | bytes 3145736 | tf_op jit(solution)/shard_map/ppermute | solution.py:23
  879.5 106.0 %collective-permute-start.18 = (bf16[256,16,128]{0,2,1:T(8,128)(2,1)}, bf16[256,16,128]{0,2,1:T(8,128)(2,1)}, u32[]{:S(2)}, u32[]{:S(2)}) collective-permute-start(bf16[256,16,128]{0,2,1:T(8,128)(2,1)} %bitcast.803), channel_id=1, source_target_pairs={{0,2},{1,3},{2,4},{3,5},{4,6},{5,7},{8,10},{9,11},{10,12},{11,13},... | collective-permute-start | bytes 3145736 | tf_op jit(solution)/shard_map/ppermute | solution.py:23
  880.9 110.0 %collective-permute-start.19 = (bf16[256,16,128]{0,2,1:T(8,128)(2,1)}, bf16[256,16,128]{0,2,1:T(8,128)(2,1)}, u32[]{:S(2)}, u32[]{:S(2)}) collective-permute-start(bf16[256,16,128]{0,2,1:T(8,128)(2,1)} %bitcast.804), channel_id=1, source_target_pairs={{0,1},{1,2},{2,3},{3,4},{4,5},{5,6},{6,7},{8,9},{9,10},{10,11},{11... | collective-permute-start | bytes 3145736 | tf_op jit(solution)/shard_map/ppermute | solution.py:23
  895.2 97.1 %collective-permute-start.20 = (bf16[256,16,128]{2,0,1:T(8,128)(2,1)}, bf16[256,16,128]{2,0,1:T(8,128)(2,1)}, u32[]{:S(2)}, u32[]{:S(2)}) collective-permute-start(bf16[256,16,128]{2,0,1:T(8,128)(2,1)} %bitcast.766), channel_id=1, source_target_pairs={{0,4},{1,5},{2,6},{3,7},{8,12},{9,13},{10,14},{11,15}} | collective-permute-start | bytes 3145736 | tf_op jit(solution)/shard_map/ppermute | solution.py:23
  1112.5 81.5 %collective-permute-start.24 = (bf16[256,16,128]{0,2,1:T(8,128)(2,1)}, bf16[256,16,128]{0,2,1:T(8,128)(2,1)S(1)}, u32[]{:S(2)}, u32[]{:S(2)}) collective-permute-start(bf16[256,16,128]{0,2,1:T(8,128)(2,1)} %bitcast.806), channel_id=1, source_target_pairs={{0,4},{1,5},{2,6},{3,7},{8,12},{9,13},{10,14},{11,15}} | collective-permute-start | bytes 3145736 | tf_op jit(solution)/shard_map/ppermute | solution.py:23
  1113.8 83.0 %collective-permute-start.25 = (bf16[256,16,128]{0,2,1:T(8,128)(2,1)}, bf16[256,16,128]{0,2,1:T(8,128)(2,1)S(1)}, u32[]{:S(2)}, u32[]{:S(2)}) collective-permute-start(bf16[256,16,128]{0,2,1:T(8,128)(2,1)} %bitcast.807), channel_id=1, source_target_pairs={{0,3},{1,4},{2,5},{3,6},{4,7},{8,11},{9,12},{10,13},{11,14},{12,15}} | collective-permute-start | bytes 3145736 | tf_op jit(solution)/shard_map/ppermute | solution.py:23
  1115.1 105.3 %collective-permute-start.26 = (bf16[256,16,128]{0,2,1:T(8,128)(2,1)}, bf16[256,16,128]{0,2,1:T(8,128)(2,1)}, u32[]{:S(2)}, u32[]{:S(2)}) collective-permute-start(bf16[256,16,128]{0,2,1:T(8,128)(2,1)} %bitcast.808), channel_id=1, source_target_pairs={{0,2},{1,3},{2,4},{3,5},{4,6},{5,7},{8,10},{9,11},{10,12},{11,13},... | collective-permute-start | bytes 3145736 | tf_op jit(solution)/shard_map/ppermute | solution.py:23
  1116.4 109.2 %collective-permute-start.27 = (bf16[256,16,128]{0,2,1:T(8,128)(2,1)}, bf16[256,16,128]{0,2,1:T(8,128)(2,1)}, u32[]{:S(2)}, u32[]{:S(2)}) collective-permute-start(bf16[256,16,128]{0,2,1:T(8,128)(2,1)} %bitcast.809), channel_id=1, source_target_pairs={{0,1},{1,2},{2,3},{3,4},{4,5},{5,6},{6,7},{8,9},{9,10},{10,11},{11... | collective-permute-start | bytes 3145736 | tf_op jit(solution)/shard_map/ppermute | solution.py:23
  1130.5 97.9 %collective-permute-start.28 = (bf16[256,16,128]{2,0,1:T(8,128)(2,1)}, bf16[256,16,128]{2,0,1:T(8,128)(2,1)}, u32[]{:S(2)}, u32[]{:S(2)}) collective-permute-start(bf16[256,16,128]{2,0,1:T(8,128)(2,1)} %bitcast.765), channel_id=1, source_target_pairs={{0,4},{1,5},{2,6},{3,7},{8,12},{9,13},{10,14},{11,15}} | collective-permute-start | bytes 3145736 | tf_op jit(solution)/shard_map/ppermute | solution.py:23
  1348.9 79.9 %collective-permute-start.32 = (bf16[256,16,128]{0,2,1:T(8,128)(2,1)}, bf16[256,16,128]{0,2,1:T(8,128)(2,1)S(1)}, u32[]{:S(2)}, u32[]{:S(2)}) collective-permute-start(bf16[256,16,128]{0,2,1:T(8,128)(2,1)} %bitcast.811), channel_id=1, source_target_pairs={{0,4},{1,5},{2,6},{3,7},{8,12},{9,13},{10,14},{11,15}} | collective-permute-start | bytes 3145736 | tf_op jit(solution)/shard_map/ppermute | solution.py:23
  1350.2 82.3 %collective-permute-start.33 = (bf16[256,16,128]{0,2,1:T(8,128)(2,1)}, bf16[256,16,128]{0,2,1:T(8,128)(2,1)S(1)}, u32[]{:S(2)}, u32[]{:S(2)}) collective-permute-start(bf16[256,16,128]{0,2,1:T(8,128)(2,1)} %bitcast.812), channel_id=1, source_target_pairs={{0,3},{1,4},{2,5},{3,6},{4,7},{8,11},{9,12},{10,13},{11,14},{12,15}} | collective-permute-start | bytes 3145736 | tf_op jit(solution)/shard_map/ppermute | solution.py:23
  1351.5 104.6 %collective-permute-start.34 = (bf16[256,16,128]{0,2,1:T(8,128)(2,1)}, bf16[256,16,128]{0,2,1:T(8,128)(2,1)}, u32[]{:S(2)}, u32[]{:S(2)}) collective-permute-start(bf16[256,16,128]{0,2,1:T(8,128)(2,1)} %bitcast.813), channel_id=1, source_target_pairs={{0,2},{1,3},{2,4},{3,5},{4,6},{5,7},{8,10},{9,11},{10,12},{11,13},... | collective-permute-start | bytes 3145736 | tf_op jit(solution)/shard_map/ppermute | solution.py:23
  1352.8 108.6 %collective-permute-start.35 = (bf16[256,16,128]{0,2,1:T(8,128)(2,1)}, bf16[256,16,128]{0,2,1:T(8,128)(2,1)}, u32[]{:S(2)}, u32[]{:S(2)}) collective-permute-start(bf16[256,16,128]{0,2,1:T(8,128)(2,1)} %bitcast.814), channel_id=1, source_target_pairs={{0,1},{1,2},{2,3},{3,4},{4,5},{5,6},{6,7},{8,9},{9,10},{10,11},{11... | collective-permute-start | bytes 3145736 | tf_op jit(solution)/shard_map/ppermute | solution.py:23
  1366.9 96.4 %collective-permute-start.36 = (bf16[256,16,128]{2,0,1:T(8,128)(2,1)}, bf16[256,16,128]{2,0,1:T(8,128)(2,1)}, u32[]{:S(2)}, u32[]{:S(2)}) collective-permute-start(bf16[256,16,128]{2,0,1:T(8,128)(2,1)} %bitcast.764), channel_id=1, source_target_pairs={{0,4},{1,5},{2,6},{3,7},{8,12},{9,13},{10,14},{11,15}} | collective-permute-start | bytes 3145736 | tf_op jit(solution)/shard_map/ppermute | solution.py:23
  1770.4 128.1 %collective-permute-start.53 = (bf16[256,16,128]{2,0,1:T(8,128)(2,1)}, bf16[256,16,128]{2,0,1:T(8,128)(2,1)}, u32[]{:S(2)}, u32[]{:S(2)}) collective-permute-start(bf16[256,16,128]{2,0,1:T(8,128)(2,1)} %collective-permute-done.51), channel_id=1, source_target_pairs={{0,1},{1,2},{2,3},{3,4},{4,5},{5,6},{6,7},{7,0},{8,9},{9,10},{10,1... | collective-permute-start | bytes 3145736 | tf_op jit(solution)/shard_map/ppermute | solution.py:101
  1781.6 116.9 %collective-permute-start.52 = (bf16[256,16,128]{2,0,1:T(8,128)(2,1)}, bf16[256,16,128]{2,0,1:T(8,128)(2,1)}, u32[]{:S(2)}, u32[]{:S(2)}) collective-permute-start(bf16[256,16,128]{2,0,1:T(8,128)(2,1)} %collective-permute-done.50), channel_id=1, source_target_pairs={{0,1},{1,2},{2,3},{3,4},{4,5},{5,6},{6,7},{7,0},{8,9},{9,10},{10,1... | collective-permute-start | bytes 3145736 | tf_op jit(solution)/shard_map/ppermute | solution.py:100
  (82 other events, 3189.6 us)
where the time goes:
time: 1960 us; the launch traced here: 1950 us
  local copies, waits for them, and re-layouts  651 us (33%)
  matrix products  642 us (33%)
  waiting for transfers between devices  469 us (24%)
  starting transfers between devices  157 us (8%)
  other arithmetic  27.2 us (1%)
    ppermute x40, waiting for transfers between devices, earlier_keys(): pieces.append(lax.ppermute(src, 'cp', [(s, s + j) for s in range(n - j)]))  382 us
    slice x1, local copies, waits for them, and re-layouts, body(): wq[layer].reshape(dm, heads * hd)  171 us
    slice x1, local copies, waits for them, and re-layouts, body(): wo[layer].reshape(heads * hd, dm)  170 us
    dot_general x6, matrix products, body(): jnp.dot(o, wo[layer].reshape(heads * hd, dm), preferred_element_type=jnp....  131 us
    sub x5, matrix products, block(): pr = jnp.where(mask, jnp.exp(s - mx), 0.0)  119 us
    dot_general x6, matrix products, body(): jnp.dot(h, wq[layer].reshape(dm, heads * hd), preferred_element_type=jnp....  114 us
    slice x1, local copies, waits for them, and re-layouts, body(): wv[layer].reshape(dm, kvh * hd)  86.3 us
    slice x1, local copies, waits for them, and re-layouts, body(): wk[layer].reshape(dm, kvh * hd)  86.1 us
  transfers between devices with their start and end apart: 54, of which 27 were waited for; matrix products, arithmetic and copies ran while one was open for 40% of the time, Pallas kernels for 0%

commit v1 on v0

v1 whole, which is shorter than its diff:
```python
import functools
import jax
import jax.numpy as jnp
from jax import lax
from jax.experimental import pallas as pl
from jax.experimental.pallas import tpu as pltpu
from jax.sharding import PartitionSpec as P

F32 = jnp.float32
BF16 = jnp.bfloat16
LAYERS, D, HEADS, KVH, HD = 6, 5376, 32, 16, 128
T = 256
PT = 2 * T
QB = 256
KC = 1792
KS = 256
WN = 768
NW = D // WN
WSLOTS = 3
CW = 1024
G = 2
GW = CW // G
HPG = 8 // G
NEG = -1e30
CSCALE = (HD ** -0.5) * 1.4426950408889634
PIECES = [(t, g) for g in range(G) for t in (0, 1)]


def kernel(x_hbm, wq, wk, wv, wo, out, x, h, kv, q, orecv, acc, wa, wb, m_s, l_s, a_s,
           sx, swa, swb, hs, hr, osd, orv, ks, kr, so, credit):
    r = lax.axis_index('cp')
    c = r // 2
    k = r % 2
    mate = r + 1 - 2 * k
    own = pl.multiple_of(k * T, T)
    oth = pl.multiple_of((1 - k) * T, T)
    row0 = pl.multiple_of(c * PT, PT)

    barrier = pltpu.get_barrier_semaphore()
    for d in range(1, 8):
        pl.semaphore_signal(barrier, inc=1, device_id={'cp': (r + d) % 8})
    pl.semaphore_wait(barrier, 7)

    def wa_copy(l, g, kc, which):
        rows = pl.ds(kc * KC, KC)
        if which == 0:
            src = wk.at[l, rows, pl.ds(pl.multiple_of(k * 8, 8), 8), :]
        elif which == 1:
            src = wv.at[l, rows, pl.ds(pl.multiple_of(k * 8, 8), 8), :]
        else:
            src = wq.at[l, rows, pl.ds(pl.multiple_of(k * 16 + (g - 2) * 8, 8), 8), :]
        return pltpu.make_async_copy(src, wa.at[kc], swa.at[kc])

    def wa_start(l, g, kc):
        @pl.when(g == 0)
        def _():
            wa_copy(l, g, kc, 0).start()

        @pl.when(g == 1)
        def _():
            wa_copy(l, g, kc, 1).start()

        @pl.when(g >= 2)
        def _():
            wa_copy(l, g, kc, 2).start()

    def wb_copy(l, n, slot):
        cols = pl.ds(pl.multiple_of(n * WN, WN), WN)
        return pltpu.make_async_copy(wo.at[l, :, :, cols], wb.at[slot], swb.at[slot])

    xin = pltpu.make_async_copy(x_hbm, x, sx)
    xin.start()
    for kc in range(3):
        wa_copy(0, 0, kc, 0).start()
    for n in range(WSLOTS):
        wb_copy(0, n, n).start()
    xin.wait()

    def x_send(n):
        cols = pl.ds(pl.multiple_of(n * WN, WN), WN)
        return pltpu.make_async_remote_copy(x.at[:, cols], h.at[pl.ds(own, T), cols], hs.at[n], hr.at[n],
                                            device_id={'cp': mate})

    def o_send(p):
        cols = pl.ds(p * 1024, 1024)
        return pltpu.make_async_remote_copy(q.at[pl.ds(oth, T), cols], orecv.at[:, cols], osd.at[p], orv.at[p],
                                            device_id={'cp': mate})

    def kv_copy(par, t, g, slot, chip, idx):
        piece = kv.at[par, t, pl.ds(pl.multiple_of(slot * PT, PT), PT), pl.ds(g * GW, GW)]
        return pltpu.make_async_remote_copy(piece, piece, ks.at[par, t, g, idx], kr.at[par, t, g, slot],
                                            device_id={'cp': 2 * chip + k})

    def kv_sends(l, par, t, g, act):
        @pl.when(c == 0)
        def _():
            act(kv_copy(par, t, g, 0, 1, 0))
            act(kv_copy(par, t, g, 0, 2, 1))

        @pl.when((c == 0) & (l == LAYERS - 1))
        def _():
            act(kv_copy(par, t, g, 0, 3, 2))

        @pl.when((c == 1) | (c == 2))
        def _():
            act(kv_copy(par, t, g, c, 3, 0))

    def start(cp):
        cp.start()

    def wait_send(cp):
        cp.wait_send()

    def kv_wait_recv(par, t, g, slot):
        kv_copy(par, t, g, slot, c, 0).wait_recv()

    def credits_wait():
        @pl.when(c <= 2)
        def _():
            pl.semaphore_wait(credit.at[0], 1)

        @pl.when(c == 0)
        def _():
            pl.semaphore_wait(credit.at[1], 1)

    def credits_give():
        def give(chip, idx):
            pl.semaphore_signal(credit.at[idx], inc=1, device_id={'cp': 2 * chip + k})

        @pl.when(c == 1)
        def _():
            give(0, 0)

        @pl.when(c == 2)
        def _():
            give(0, 1)
            give(3, 1)

        @pl.when(c == 3)
        def _():
            give(1, 0)
            give(2, 0)

    def relay(l, t, g, first):
        par = l % 2

        @pl.when((c == 3) & (l < LAYERS))
        def _():
            if first:
                @pl.when(l >= 2)
                def _():
                    pl.semaphore_wait(credit.at[1], 1)
            kv_wait_recv(par, t, g, 1)
            kv_copy(par, t, g, 1, 2, 1).start()

    def relay_wait(l):
        par = l % 2

        @pl.when(c == 3)
        def _():
            for t, g in PIECES:
                kv_copy(par, t, g, 1, 2, 1).wait_send()

    rowi = lax.broadcasted_iota(jnp.int32, (2 * QB, QB), 0) % QB
    coli = lax.broadcasted_iota(jnp.int32, (2 * QB, QB), 1)

    def tile(par, j, b, kb, mode, first):
        jq = pl.multiple_of(j * 256, 256)
        rows = pl.ds(b * QB, QB)
        kcols = pl.ds(pl.multiple_of(j * HD, HD), HD)
        krows = pl.ds(pl.multiple_of(kb * QB, QB), QB)
        qq = jnp.concatenate([q[rows, pl.ds(jq, HD)], q[rows, pl.ds(pl.multiple_of(jq + HD, HD), HD)]], axis=0)
        s = lax.dot_general(qq, kv[par, 0, krows, kcols], (((1,), (1,)), ((), ())), preferred_element_type=F32)
        s = s * CSCALE
        if mode == 'diag':
            s = jnp.where(coli <= rowi, s, NEG)
        elif mode == 'old':
            s = jnp.where(coli > rowi, s, NEG)
        mx = jnp.max(s, axis=1, keepdims=True)
        v = kv[par, 1, krows, kcols]
        if first:
            mn = jnp.broadcast_to(mx, (2 * QB, HD))
            p = jnp.exp2(s - jnp.concatenate([mn, mn], axis=1))
            l_s[b] = p[:, :HD] + p[:, HD:]
            a_s[b] = jnp.dot(p.astype(BF16), v, preferred_element_type=F32)
        else:
            mo = m_s[b]
            mn = jnp.maximum(mo, mx)
            p = jnp.exp2(s - jnp.concatenate([mn, mn], axis=1))
            al = jnp.exp2(mo - mn)
            l_s[b] = l_s[b] * al + (p[:, :HD] + p[:, HD:])
            a_s[b] = a_s[b] * al + jnp.dot(p.astype(BF16), v, preferred_element_type=F32)
        m_s[b] = mn

    def attention(l, par):
        last = l == LAYERS - 1

        def head(j, _):
            @pl.when(j % HPG == 0)
            def _():
                g = j // HPG
                for s in range(3):
                    @pl.when((s < c) & ((s >= c - 2) | last) & ((c != 3) | (s != 1)))
                    def _():
                        for t in (0, 1):
                            kv_dyn_wait(par, t, g, s)
            for b in (0, 1):
                tile(par, j, b, 2 * c + b, 'diag', True)
            hi = jnp.where(last, 2 * c, jnp.minimum(3, 2 * c))

            def mid(t, _):
                for b in (0, 1):
                    tile(par, j, b, 2 * c + b - t, 'mid', False)
                return 0

            lax.fori_loop(1, hi + 1, mid, 0)

            @pl.when(last | (c <= 1))
            def _():
                tile(par, j, 1, 0, 'mid', False)

            @pl.when((c >= 2) & jnp.logical_not(last))
            def _():
                for b in (0, 1):
                    tile(par, j, b, 2 * c + b - 4, 'old', False)
            jq = pl.multiple_of(j * 256, 256)
            for b in (0, 1):
                o = a_s[b] / jnp.sum(l_s[b], axis=1, keepdims=True)
                o = o.astype(BF16)
                q[b * QB:(b + 1) * QB, pl.ds(jq, HD)] = o[:QB]
                q[b * QB:(b + 1) * QB, pl.ds(pl.multiple_of(jq + HD, HD), HD)] = o[QB:]

            @pl.when(j == 4)
            def _():
                o_send(0).start()
            return 0

        lax.fori_loop(0, 8, head, 0)
        o_send(1).start()

    def kv_dyn_wait(par, t, g, slot):
        piece = kv.at[par, t, pl.ds(slot * PT, PT), pl.ds(pl.multiple_of(g * GW, GW), GW)]
        pltpu.make_async_remote_copy(piece, piece, ks.at[par, t, g, 0], kr.at[par, t, g, slot],
                                     device_id={'cp': mate}).wait_recv()

    def norm_rows(src, dst, r0):
        def blk(i, _):
            rows = pl.ds(pl.multiple_of(r0 + i * 16, 16), 16)
            srows = rows if src is h else pl.ds(pl.multiple_of(i * 16, 16), 16)
            xf = src[srows, :].astype(F32)
            ms = jnp.mean(xf * xf, axis=-1, keepdims=True)
            dst[rows, :] = (xf * lax.rsqrt(ms + 1e-6)).astype(BF16)
            return 0
        lax.fori_loop(0, T // 16, blk, 0)

    for n in range(NW):
        x_send(n).start()

    def layer(l, _):
        par = l % 2
        norm_rows(x, h, own)
        for n in range(NW):
            x_send(n).wait()
        norm_rows(h, h, oth)

        @pl.when(l >= 2)
        def _():
            for t, g in PIECES:
                kv_sends(l - 2, par, t, g, wait_send)
            credits_wait()

        def group(g, _):
            for kc in range(3):
                wa_copy(l, g, kc, 0).wait()
                for s in range(KC // KS):
                    w = wa[kc, s * KS:(s + 1) * KS].reshape(KS, CW)
                    o = kc * KC + s * KS
                    p = jnp.dot(h[:, o:o + KS], w, preferred_element_type=F32)
                    if o == 0:
                        acc[...] = p
                    else:
                        acc[...] += p

                @pl.when(g < 3)
                def _():
                    wa_start(l, g + 1, kc)

                @pl.when((g == 3) & (l < LAYERS - 1))
                def _():
                    wa_copy(l + 1, 0, kc, 0).start()

                if kc == 0:
                    @pl.when(g == 1)
                    def _():
                        kv_sends(l, par, 0, 0, start)

                    @pl.when(g == 2)
                    def _():
                        kv_sends(l, par, 1, 0, start)
                        for gg in range(1, G):
                            kv_sends(l, par, 0, gg, start)
                            kv_sends(l, par, 1, gg, start)

            @pl.when(g == 0)
            def _():
                kv[par, 0, pl.ds(row0, PT), :] = acc[...].astype(BF16)

            @pl.when(g == 1)
            def _():
                kv[par, 1, pl.ds(row0, PT), :] = acc[...].astype(BF16)

            @pl.when(g >= 2)
            def _():
                q[:, pl.ds(pl.multiple_of((g - 2) * CW, CW), CW)] = acc[...].astype(BF16)

            @pl.when((g == 0) & (l >= 1))
            def _():
                relay(l, 1, 1, False)
            return 0

        @pl.when(l >= 1)
        def _():
            for p in range(2):
                o_send(p).wait_send()
        lax.fori_loop(0, 4, group, 0)

        @pl.when(l == 0)
        def _():
            for i, (t, g) in enumerate(PIECES):
                relay(l, t, g, i == 0)
        relay(l + 1, 0, 0, True)

        attention(l, par)
        relay_wait(l)

        @pl.when(l <= LAYERS - 3)
        def _():
            credits_give()
        relay(l + 1, 1, 0, False)
        for p in range(2):
            o_send(p).wait_recv()

        def chunk(n, _):
            slot = (l * NW + n) % WSLOTS
            wb_copy(l, n, slot).wait()
            cols = pl.ds(pl.multiple_of(n * WN, WN), WN)
            wown = wb[slot, pl.ds(k * 16, 16)].reshape(2048, WN)
            woth = wb[slot, pl.ds((1 - k) * 16, 16)].reshape(2048, WN)
            y = jnp.dot(q[pl.ds(own, T), :], wown, preferred_element_type=F32)
            y = y + jnp.dot(orecv[...], woth, preferred_element_type=F32)
            x[:, cols] = (x[:, cols].astype(F32) + y).astype(BF16)

            @pl.when(n + WSLOTS < NW)
            def _():
                wb_copy(l, n + WSLOTS, slot).start()

            @pl.when((n + WSLOTS >= NW) & (l < LAYERS - 1))
            def _():
                wb_copy(l + 1, n + WSLOTS - NW, slot).start()

            @pl.when((n > 0) & (l < LAYERS - 1))
            def _():
                x_send(n - 1).start()
            return 0

        lax.fori_loop(0, NW, chunk, 0)

        @pl.when(l < LAYERS - 1)
        def _():
            x_send(NW - 1).start()
        relay(l + 1, 0, 1, False)
        return 0

    lax.fori_loop(0, LAYERS, layer, 0)

    res = pltpu.make_async_copy(x, out, so)
    res.start()
    for p in range(2):
        o_send(p).wait_send()
    for l in (LAYERS - 2, LAYERS - 1):
        for t, g in PIECES:
            kv_sends(l, l % 2, t, g, wait_send)
    res.wait()


def solution(mesh):
    def body(x, wq, wk, wv, wo):
        anyspec = pl.BlockSpec(memory_space=pl.ANY)
        dma = pltpu.SemaphoreType.DMA
        return pl.pallas_call(
            kernel,
            out_shape=jax.ShapeDtypeStruct((T, D), BF16),
            in_specs=[anyspec] * 5,
            out_specs=anyspec,
            scratch_shapes=[
                pltpu.VMEM((T, D), BF16),
                pltpu.VMEM((PT, D), BF16),
                pltpu.VMEM((2, 2, 4 * PT, CW), BF16),
                pltpu.VMEM((PT, 2048), BF16),
                pltpu.VMEM((T, 2048), BF16),
                pltpu.VMEM((PT, CW), F32),
                pltpu.VMEM((3, KC, 8, HD), BF16),
                pltpu.VMEM((WSLOTS, HEADS, HD, WN), BF16),
                pltpu.VMEM((2, PT, HD), F32),
                pltpu.VMEM((2, PT, HD), F32),
                pltpu.VMEM((2, PT, HD), F32),
                dma, dma((3,)), dma((WSLOTS,)), dma((NW,)), dma((NW,)), dma((2,)), dma((2,)),
                dma((2, 2, G, 3)), dma((2, 2, G, 4)), dma,
                pltpu.SemaphoreType.REGULAR((2,)),
            ],
            compiler_params=pltpu.CompilerParams(collective_id=0, has_side_effects=True,
                                                 vmem_limit_bytes=67043328),
            cost_estimate=pl.CostEstimate(flops=240 * 10 ** 9, bytes_accessed=530 * 10 ** 6, transcendentals=0),
        )(x, wq, wk, wv, wo)

    spec_x = P(('dp', 'cp'), None)
    return jax.shard_map(body, mesh=mesh, in_specs=(spec_x, P(), P(), P(), P()), out_specs=spec_x, check_vma=False)
```

time: 1960 us -> 549 us (0.28)
  local copies, waits for them, and re-layouts: 651 us -> 3.49 us
  matrix products: 642 us -> 0 us
  Pallas kernels: 0 us -> 545 us
  waiting for transfers between devices: 469 us -> 0 us
  starting transfers between devices: 157 us -> 0 us
  other arithmetic: 27.2 us -> 0 us
    pallas_call x0 -> x1, Pallas kernels: none -> 545 us  [body(): pl.pallas_call(kernel, out_shape=jax.ShapeDtypeStruct((T, D), BF16), in_s...]
    dot_general x45 -> x0, matrix products: 523 us -> none  [the longest x6 131 us: body(): jnp.dot(o, wo[layer].reshape(heads * hd, dm), preferred_element_type=jnp....]
    slice x4 -> x0, local copies, waits for them, and re-layouts: 513 us -> none  [the longest x1 171 us: body(): wq[layer].reshape(dm, heads * hd)]
    ppermute x54 -> x0, waiting for transfers between devices: 469 us -> none  [the longest x40 382 us: earlier_keys(): pieces.append(lax.ppermute(src, 'cp', [(s, s + j) for s in range(n - j)]))]
    ppermute x54 -> x0, starting transfers between devices: 157 us -> none  [the longest x7 74.8 us: global_attention(): vb = lax.ppermute(vb, 'cp', perm)]
    sub x5 -> x0, matrix products: 119 us -> none  [block(): pr = jnp.where(mask, jnp.exp(s - mx), 0.0)]
    unnamed x134 -> x1, local copies, waits for them, and re-layouts: 82.4 us -> 3.49 us
    reduce_sum x9 -> x0, other arithmetic: 20.3 us -> none  [the longest x8 19.7 us: block(): ln = alpha * lb + pr.sum(axis=-1)]
  transfers between devices with their start and end apart: 54 -> 0, of which waited for: 27 -> 0; matrix products, arithmetic and copies ran while one was open for 40% -> 0% of each run, Pallas kernels for 0% -> 0%
where the time goes in v1:
time: 549 us
  Pallas kernels  545 us (99%)
    pallas_call x1, Pallas kernels, body(): pl.pallas_call(kernel, out_shape=jax.ShapeDtypeStruct((T, D), BF16), in_s...  545 us

profile of v1, /device:TPU:7, one launch (start us, length us, event | category | flops | bytes accessed | tf_op | source)
XLA Modules:
  0.0 548.7 jit_solution(7656386605282218371)
XLA Ops:
  0.0 545.2 %shard_map.55 = bf16[256,5376]{1,0:T(8,128)(2,1)} custom-call(bf16[256,5376]{1,0:T(8,128)(2,1)} %x_hbm.1, bf16[6,5376,32,128]{3,2,1,0:T(8,128)(2,1)} %wq.1, bf16[6,5376,16,128]{3,2,1,0:T(8,128)(2,1)} %wk.1, bf16[6,5376,16,128]{3,2,1,0:T(8,128)(2,1)} %wv.1, bf16[6,32,128,5376]{3,2,1,0:T(8,128)(2,1)} %wo.1), custom_call_target="tpu_custom_call" | custom-call | flops 240000008192 | bytes 530000000 | tf_op jit(solution)/shard_map/pallas_call | solution.py:390
  545.2 3.5 copy.7

commit v2 on v1

--- a/solution.py
+++ b/solution.py
@@ -18,15 +18,15 @@
 NW = D // WN
 WSLOTS = 3
 CW = 1024
-G = 2
+G = 4
 GW = CW // G
 HPG = 8 // G
 NEG = -1e30
 CSCALE = (HD ** -0.5) * 1.4426950408889634
-PIECES = [(t, g) for g in range(G) for t in (0, 1)]
-
-
-def kernel(x_hbm, wq, wk, wv, wo, out, x, h, kv, q, orecv, acc, wa, wb, m_s, l_s, a_s,
+PIECES = [(0, 0), (0, 1), (1, 0), (1, 1), (0, 2), (1, 2), (0, 3), (1, 3)]
+
+
+def kernel(x_hbm, wq, wk, wv, wo, out, x, h, kb_, vb_, q, orecv, acc, wa, wb, m_s, l_s, a_s, s_s,
            sx, swa, swb, hs, hr, osd, orv, ks, kr, so, credit):
     r = lax.axis_index('cp')
     c = r // 2
@@ -86,8 +86,13 @@
         return pltpu.make_async_remote_copy(q.at[pl.ds(oth, T), cols], orecv.at[:, cols], osd.at[p], orv.at[p],
                                             device_id={'cp': mate})
 
+    def kv_piece(par, t, g, slot):
+        if t == 0:
+            return kb_.at[par, g, pl.ds(pl.multiple_of(slot * PT, PT), PT), :]
+        return vb_.at[par, slot, pl.ds(pl.multiple_of(g * GW, GW), GW), :]
+
     def kv_copy(par, t, g, slot, chip, idx):
-        piece = kv.at[par, t, pl.ds(pl.multiple_of(slot * PT, PT), PT), pl.ds(g * GW, GW)]
+        piece = kv_piece(par, t, g, slot)
         return pltpu.make_async_remote_copy(piece, piece, ks.at[par, t, g, idx], kr.at[par, t, g, slot],
                                             device_id={'cp': 2 * chip + k})
 
@@ -97,13 +102,12 @@
             act(kv_copy(par, t, g, 0, 1, 0))
             act(kv_copy(par, t, g, 0, 2, 1))
 
-        @pl.when((c == 0) & (l == LAYERS - 1))
-        def _():
-            act(kv_copy(par, t, g, 0, 3, 2))
-
         @pl.when((c == 1) | (c == 2))
         def _():
             act(kv_copy(par, t, g, c, 3, 0))
+
+    def kv_far(par, t, g):
+        return kv_copy(par, t, g, 0, 3, 2)
 
     def start(cp):
         cp.start()
@@ -141,12 +145,12 @@
             give(1, 0)
             give(2, 0)
 
-    def relay(l, t, g, first):
+    def relay(l, t, g):
         par = l % 2
 
         @pl.when((c == 3) & (l < LAYERS))
         def _():
-            if first:
+            if (t, g) == PIECES[0]:
                 @pl.when(l >= 2)
                 def _():
                     pl.semaphore_wait(credit.at[1], 1)
@@ -161,36 +165,52 @@
             for t, g in PIECES:
                 kv_copy(par, t, g, 1, 2, 1).wait_send()
 
-    rowi = lax.broadcasted_iota(jnp.int32, (2 * QB, QB), 0) % QB
-    coli = lax.broadcasted_iota(jnp.int32, (2 * QB, QB), 1)
-
-    def tile(par, j, b, kb, mode, first):
+    keyi = lax.broadcasted_iota(jnp.int32, (QB, 2 * QB), 0)
+    qryi = lax.broadcasted_iota(jnp.int32, (QB, 2 * QB), 1) % QB
+
+    def score(par, j, b, kb, mode, slot):
         jq = pl.multiple_of(j * 256, 256)
         rows = pl.ds(b * QB, QB)
-        kcols = pl.ds(pl.multiple_of(j * HD, HD), HD)
+        kcols = pl.ds(pl.multiple_of((j % HPG) * HD, HD), HD)
         krows = pl.ds(pl.multiple_of(kb * QB, QB), QB)
         qq = jnp.concatenate([q[rows, pl.ds(jq, HD)], q[rows, pl.ds(pl.multiple_of(jq + HD, HD), HD)]], axis=0)
-        s = lax.dot_general(qq, kv[par, 0, krows, kcols], (((1,), (1,)), ((), ())), preferred_element_type=F32)
+        s = lax.dot_general(kb_[par, j // HPG, krows, kcols], qq, (((1,), (1,)), ((), ())), preferred_element_type=F32)
         s = s * CSCALE
         if mode == 'diag':
-            s = jnp.where(coli <= rowi, s, NEG)
+            s = jnp.where(keyi <= qryi, s, NEG)
         elif mode == 'old':
-            s = jnp.where(coli > rowi, s, NEG)
-        mx = jnp.max(s, axis=1, keepdims=True)
-        v = kv[par, 1, krows, kcols]
+            s = jnp.where(keyi > qryi, s, NEG)
+        s_s[slot] = s
+        return jnp.max(s, axis=0, keepdims=True)
+
+    def consume(par, j, b, kb, mx, slot, first):
+        kcols = pl.ds(pl.multiple_of(j * HD, HD), HD)
+        v = vb_[par, kb // 2, kcols, pl.ds(pl.multiple_of((kb % 2) * QB, QB), QB)]
         if first:
-            mn = jnp.broadcast_to(mx, (2 * QB, HD))
-            p = jnp.exp2(s - jnp.concatenate([mn, mn], axis=1))
-            l_s[b] = p[:, :HD] + p[:, HD:]
-            a_s[b] = jnp.dot(p.astype(BF16), v, preferred_element_type=F32)
+            p = jnp.exp2(s_s[slot] - mx)
+            l_s[b] = jnp.sum(p, axis=0, keepdims=True)
+            a_s[b] = jnp.dot(v, p.astype(BF16), preferred_element_type=F32)
+            m_s[b] = mx
         else:
             mo = m_s[b]
             mn = jnp.maximum(mo, mx)
-            p = jnp.exp2(s - jnp.concatenate([mn, mn], axis=1))
+            p = jnp.exp2(s_s[slot] - mn)
             al = jnp.exp2(mo - mn)
-            l_s[b] = l_s[b] * al + (p[:, :HD] + p[:, HD:])
-            a_s[b] = a_s[b] * al + jnp.dot(p.astype(BF16), v, preferred_element_type=F32)
-        m_s[b] = mn
+            l_s[b] = l_s[b] * al + jnp.sum(p, axis=0, keepdims=True)
+            a_s[b] = a_s[b] * al + jnp.dot(v, p.astype(BF16), preferred_element_type=F32)
+            m_s[b] = mn
+
+    def tiles(par, j, items):
+        mx = None
+        for i in range(len(items) + 1):
+            nxt = None
+            if i < len(items):
+                b, kb, mode, first = items[i]
+                nxt = score(par, j, b, kb, mode, i % 2)
+            if i > 0:
+                b, kb, mode, first = items[i - 1]
+                consume(par, j, b, kb, mx, (i - 1) % 2, first)
+            mx = nxt
 
     def attention(l, par):
         last = l == LAYERS - 1
@@ -200,33 +220,32 @@
             def _():
                 g = j // HPG
                 for s in range(3):
-                    @pl.when((s < c) & ((s >= c - 2) | last) & ((c != 3) | (s != 1)))
+                    @pl.when((s < c) & ((s >= c - 2) | last) & ((c != 3) | (s != 1))
+                             & ((c != 2) | (s != 0) | jnp.logical_not(last) | (g >= 2)))
                     def _():
                         for t in (0, 1):
                             kv_dyn_wait(par, t, g, s)
-            for b in (0, 1):
-                tile(par, j, b, 2 * c + b, 'diag', True)
-            hi = jnp.where(last, 2 * c, jnp.minimum(3, 2 * c))
-
-            def mid(t, _):
-                for b in (0, 1):
-                    tile(par, j, b, 2 * c + b - t, 'mid', False)
-                return 0
-
-            lax.fori_loop(1, hi + 1, mid, 0)
-
-            @pl.when(last | (c <= 1))
-            def _():
-                tile(par, j, 1, 0, 'mid', False)
-
-            @pl.when((c >= 2) & jnp.logical_not(last))
-            def _():
-                for b in (0, 1):
-                    tile(par, j, b, 2 * c + b - 4, 'old', False)
+            full = (c >= 2) & jnp.logical_not(last)
+
+            @pl.when(full)
+            def _():
+                tiles(par, j, [(b, 2 * c + b - t, ('diag', 'mid', 'mid', 'mid', 'old')[t], t == 0)
+                               for t in range(5) for b in (0, 1)])
+
+            @pl.when(jnp.logical_not(full))
+            def _():
+                tiles(par, j, [(b, 2 * c + b, 'diag', True) for b in (0, 1)])
+
+                def mid(i, _):
+                    tiles(par, j, [(b, 2 * c + b - 1 - 2 * i - u, 'mid', False) for u in (0, 1) for b in (0, 1)])
+                    return 0
+
+                lax.fori_loop(0, c, mid, 0)
+                tiles(par, j, [(1, 0, 'mid', False)])
+
             jq = pl.multiple_of(j * 256, 256)
             for b in (0, 1):
-                o = a_s[b] / jnp.sum(l_s[b], axis=1, keepdims=True)
-                o = o.astype(BF16)
+                o = (a_s[b] * (1.0 / l_s[b])).T.astype(BF16)
                 q[b * QB:(b + 1) * QB, pl.ds(jq, HD)] = o[:QB]
                 q[b * QB:(b + 1) * QB, pl.ds(pl.multiple_of(jq + HD, HD), HD)] = o[QB:]
 
@@ -239,7 +258,7 @@
         o_send(1).start()
 
     def kv_dyn_wait(par, t, g, slot):
-        piece = kv.at[par, t, pl.ds(slot * PT, PT), pl.ds(pl.multiple_of(g * GW, GW), GW)]
+        piece = kv_piece(par, t, g, slot)
         pltpu.make_async_remote_copy(piece, piece, ks.at[par, t, g, 0], kr.at[par, t, g, slot],
                                      device_id={'cp': mate}).wait_recv()
 
@@ -262,6 +281,10 @@
         for n in range(NW):
             x_send(n).wait()
         norm_rows(h, h, oth)
+
+        @pl.when(l >= 1)
+        def _():
+            relay(l, *PIECES[4])
 
         @pl.when(l >= 2)
         def _():
@@ -292,22 +315,26 @@
                 if kc == 0:
                     @pl.when(g == 1)
                     def _():
-                        kv_sends(l, par, 0, 0, start)
+                        for t, gg in PIECES[:2]:
+                            kv_sends(l, par, t, gg, start)
 
                     @pl.when(g == 2)
                     def _():
-                        kv_sends(l, par, 1, 0, start)
-                        for gg in range(1, G):
-                            kv_sends(l, par, 0, gg, start)
-                            kv_sends(l, par, 1, gg, start)
+                        for t, gg in PIECES[2:]:
+                            kv_sends(l, par, t, gg, start)
+
+                    @pl.when((g == 1) & (l >= 1))
+                    def _():
+                        relay(l, *PIECES[6])
 
             @pl.when(g == 0)
             def _():
-                kv[par, 0, pl.ds(row0, PT), :] = acc[...].astype(BF16)
+                for gg in range(G):
+                    kb_[par, gg, pl.ds(row0, PT), :] = acc[:, gg * GW:(gg + 1) * GW].astype(BF16)
 
             @pl.when(g == 1)
             def _():
-                kv[par, 1, pl.ds(row0, PT), :] = acc[...].astype(BF16)
+                vb_[par, c] = acc[...].T.astype(BF16)
 
             @pl.when(g >= 2)
             def _():
@@ -315,7 +342,11 @@
 
             @pl.when((g == 0) & (l >= 1))
             def _():
-                relay(l, 1, 1, False)
+                relay(l, *PIECES[5])
+
+            @pl.when((g == 1) & (l >= 1))
+            def _():
+                relay(l, *PIECES[7])
             return 0
 
         @pl.when(l >= 1)
@@ -326,9 +357,8 @@
 
         @pl.when(l == 0)
         def _():
-            for i, (t, g) in enumerate(PIECES):
-                relay(l, t, g, i == 0)
-        relay(l + 1, 0, 0, True)
+            for t, g in PIECES:
+                relay(l, t, g)
 
         attention(l, par)
         relay_wait(l)
@@ -336,12 +366,22 @@
         @pl.when(l <= LAYERS - 3)
         def _():
             credits_give()
-        relay(l + 1, 1, 0, False)
         for p in range(2):
             o_send(p).wait_recv()
 
         def chunk(n, _):
             slot = (l * NW + n) % WSLOTS
+            for i, at in enumerate((0, 3, 5)):
+                @pl.when(n == at)
+                def _():
+                    relay(l + 1, *PIECES[i])
+
+            @pl.when((c == 2) & (n == 3) & (l == LAYERS - 2))
+            def _():
+                for t, g in PIECES[:4]:
+                    kv_wait_recv((LAYERS - 1) % 2, t, g, 0)
+                    kv_copy((LAYERS - 1) % 2, t, g, 0, 3, 1).start()
+
             wb_copy(l, n, slot).wait()
             cols = pl.ds(pl.multiple_of(n * WN, WN), WN)
             wown = wb[slot, pl.ds(k * 16, 16)].reshape(2048, WN)
@@ -368,7 +408,7 @@
         @pl.when(l < LAYERS - 1)
         def _():
             x_send(NW - 1).start()
-        relay(l + 1, 0, 1, False)
+        relay(l + 1, *PIECES[3])
         return 0
 
     lax.fori_loop(0, LAYERS, layer, 0)
@@ -380,6 +420,18 @@
     for l in (LAYERS - 2, LAYERS - 1):
         for t, g in PIECES:
             kv_sends(l, l % 2, t, g, wait_send)
+
+    @pl.when(c == 0)
+    def _():
+        for t, g in PIECES[4:]:
+            kv_far((LAYERS - 1) % 2, t, g).start()
+        for t, g in PIECES[4:]:
+            kv_far((LAYERS - 1) % 2, t, g).wait_send()
+
+    @pl.when(c == 2)
+    def _():
+        for t, g in PIECES[:4]:
+            kv_copy((LAYERS - 1) % 2, t, g, 0, 3, 1).wait_send()
     res.wait()
 
 
@@ -395,15 +447,17 @@
             scratch_shapes=[
                 pltpu.VMEM((T, D), BF16),
                 pltpu.VMEM((PT, D), BF16),
-                pltpu.VMEM((2, 2, 4 * PT, CW), BF16),
+                pltpu.VMEM((2, G, 4 * PT, GW), BF16),
+                pltpu.VMEM((2, 4, CW, PT), BF16),
                 pltpu.VMEM((PT, 2048), BF16),
                 pltpu.VMEM((T, 2048), BF16),
                 pltpu.VMEM((PT, CW), F32),
                 pltpu.VMEM((3, KC, 8, HD), BF16),
                 pltpu.VMEM((WSLOTS, HEADS, HD, WN), BF16),
-                pltpu.VMEM((2, PT, HD), F32),
-                pltpu.VMEM((2, PT, HD), F32),
-                pltpu.VMEM((2, PT, HD), F32),
+                pltpu.VMEM((2, 1, 2 * QB), F32),
+                pltpu.VMEM((2, 1, 2 * QB), F32),
+                pltpu.VMEM((2, HD, 2 * QB), F32),
+                pltpu.VMEM((2, QB, 2 * QB), F32),
                 dma, dma((3,)), dma((WSLOTS,)), dma((NW,)), dma((NW,)), dma((2,)), dma((2,)),
                 dma((2, 2, G, 3)), dma((2, 2, G, 4)), dma,
                 pltpu.SemaphoreType.REGULAR((2,)),

time: 549 us -> 492 us (0.90)
  Pallas kernels: 545 us -> 488 us
    pallas_call x1, Pallas kernels: 545 us -> 488 us  [body(): pl.pallas_call(kernel, out_shape=jax.ShapeDtypeStruct((T, D), BF16), in_s...]
where the time goes in v2:
time: 492 us
  Pallas kernels  488 us (99%)
    pallas_call x1, Pallas kernels, body(): pl.pallas_call(kernel, out_shape=jax.ShapeDtypeStruct((T, D), BF16), in_s...  488 us

profile of v2, /device:TPU:7, one launch (start us, length us, event | category | flops | bytes accessed | tf_op | source)
XLA Modules:
  0.0 491.8 jit_solution(8363403181377136989)
XLA Ops:
  0.0 488.3 %shard_map.55 = bf16[256,5376]{1,0:T(8,128)(2,1)} custom-call(bf16[256,5376]{1,0:T(8,128)(2,1)} %x_hbm.1, bf16[6,5376,32,128]{3,2,1,0:T(8,128)(2,1)} %wq.1, bf16[6,5376,16,128]{3,2,1,0:T(8,128)(2,1)} %wk.1, bf16[6,5376,16,128]{3,2,1,0:T(8,128)(2,1)} %wv.1, bf16[6,32,128,5376]{3,2,1,0:T(8,128)(2,1)} %wo.1), custom_call_target="tpu_custom_call" | custom-call | flops 240000008192 | bytes 530000000 | tf_op jit(solution)/shard_map/pallas_call | solution.py:442
  488.3 3.5 copy.7
